TPU v7x, 256 devices: a whole 4x4x8 slice. The times are simulated.
256 devices in a mesh: expert: 16 (over z_lo, x), shard: 16 (over z_hi, y, core).
Axes of the slice: x: 4, y: 4, z: 8 (z_hi: 2, z_lo: 4; z = z_hi * 4 + z_lo), core: 2. Of those that a mesh axis runs over, the one named last changes fastest.
Arguments:
- train_down: float32 [16, 6400, 4096], P('expert', None, 'shard'), may hold values from -0.109375 to 0.109375
- router_weight: float32 [4096, 16], P('shard', 'expert'), may hold values from -0.09375 to 0.09375
- router_gain: float32 [4096], P('shard'), may hold values from 0.25 to 1.75
Outputs:
- ready_down: bfloat16 [16, 6400, 4096], P('expert', 'shard')
- scale_down: float32 [16, 6400], P('expert', 'shard')
- serve_router: bfloat16 [4096, 16], replicated
All inputs are finite; a program needn't handle non-finite values. Where the computation divides by a largest or mean magnitude, that divisor is 1e-20 or more.
Results may differ from a plain program's by a relative error of at most 0.001.
Values may be sent and summed in bfloat16 or wider, within the bound.
A program may use at most 64 MiB of HBM per device.

v0:
```python
import jax
import jax.numpy as jnp
from jax import lax
from jax.sharding import PartitionSpec as P


def from_everyone(x, axis):
    copies = jnp.broadcast_to(x, (lax.axis_size(axis), *x.shape))
    return lax.all_to_all(copies, axis, split_axis=0, concat_axis=0, tiled=True)


def taken_together(x, axis):
    everything = from_everyone(x, axis)
    return jnp.max(everything, axis=0)


def split_up(x, dim, peers):
    shape = x.shape
    blocks = x.reshape(*shape[:dim], peers, shape[dim] // peers, *shape[dim + 1 :])
    return jnp.moveaxis(blocks, dim, 0)


def edges_of(length, count):
    unit = 8 if length >= 8 * count else 1
    return [length // unit * k // count * unit for k in range(1, count)]


def laid_out(blocks, dim):
    shape = list(blocks.shape[1:])
    shape[dim] *= blocks.shape[0]
    return jnp.moveaxis(blocks, 0, dim).reshape(shape)


def exchange_in_pieces(x, axis, pieces, split_dim, concat_dim):
    blocks = split_up(x, split_dim, lax.axis_size(axis))
    split_at = max(range(1, max(2, blocks.ndim - 1)), key=lambda d: blocks.shape[d])
    gathered = []
    for piece in jnp.split(blocks, edges_of(blocks.shape[split_at], pieces), axis=split_at):
        if piece.size:
            gathered.append(lax.all_to_all(piece, axis, split_axis=0, concat_axis=0, tiled=True))
    return laid_out(jnp.concatenate(gathered, axis=split_at), concat_dim)


def collect(x, axis, dim):
    return laid_out(from_everyone(x, axis), dim)


def per_device(train_down, router_weight, router_gain):
    scale_down = taken_together(jnp.max(jnp.abs(train_down), axis=2), "shard")
    narrow_down = (train_down / jnp.expand_dims(scale_down, 2)).astype(jnp.bfloat16)
    ready_down = exchange_in_pieces(narrow_down, "shard", 2, 1, 2)
    scale_down = lax.dynamic_slice_in_dim(
        scale_down, lax.axis_index("shard") * ready_down.shape[1], ready_down.shape[1], axis=1
    )
    part_router = (router_weight * router_gain[:, None]).astype(jnp.bfloat16)
    row_router = collect(part_router, "shard", 0)
    serve_router = collect(row_router, "expert", 1)
    return (ready_down, scale_down, serve_router)


def solution(mesh):
    in_specs = (P("expert", None, "shard"), P("shard", "expert"), P("shard"))
    out_specs = (P("expert", "shard", None), P("expert", "shard"), P())
    return jax.shard_map(
        per_device, mesh=mesh, in_specs=in_specs, out_specs=out_specs, check_vma=False
    )
```

profile of v0, /device:TPU:35, one launch (start us, length us, event | category | flops | bytes accessed | tf_op | source)
XLA Modules:
  0.0 156.0 jit_solution(93651380600936288)
XLA Ops:
  0.6 0.7 convert_reduce_fusion
  1.4 0.5 broadcast.8
  1.9 0.7 reduce.6
  2.6 0.6 reshape.32
  3.2 10.9 %all-to-all-start.3 = ((bf16[16,2,128]{2,1,0:T(2,128)(2,1)}), bf16[16,2,128]{2,1,0:T(2,128)(2,1)S(1)}, u32[]{:S(2)}, u32[]{:S(2)}) async-start(bf16[16,2,128]{2,1,0:T(2,128)(2,1)} %reshape.32), calls=%async_computation.3 | async-start | bytes 16384 | tf_op jit(solution)/shard_map/all_to_all | solution.py:9
  14.1 3.8 %abs_reduce_fusion = f32[6400]{0:T(1024)S(1)} fusion(f32[1,6400,256]{2,1,0:T(8,128)} %param.3), kind=kLoop, calls=%fused_computation.1 | loop fusion | flops 3270400 | bytes 6579200 | tf_op jit(solution)/shard_map/reduce_max | solution.py:49
  17.8 5.6 %all-to-all-done.3 = bf16[16,2,128]{2,1,0:T(2,128)(2,1)S(1)} async-done(((bf16[16,2,128]{2,1,0:T(2,128)(2,1)}), bf16[16,2,128]{2,1,0:T(2,128)(2,1)S(1)}, u32[]{:S(2)}, u32[]{:S(2)}) %all-to-all-start.3) | async-done | bytes 8224 | tf_op jit(solution)/shard_map/all_to_all | solution.py:9
  23.4 1.0 broadcast_in_dim.13
  24.4 4.1 %all-to-all-start = ((f32[16,1,6400]{2,1,0:T(1,128)}), f32[16,1,6400]{2,1,0:T(1,128)S(1)}, u32[]{:S(2)}, u32[]{:S(2)}) async-start(f32[16,1,6400]{2,1,0:T(1,128)} %broadcast_in_dim.13), calls=%async_computation | async-start | bytes 819200 | tf_op jit(solution)/shard_map/all_to_all | solution.py:9
  28.5 0.1 bitcast_reduce_fusion
  28.5 0.2 broadcast_bitcast_fusion
  28.7 1.4 reduce.7
  30.1 0.7 reshape.34
  30.9 14.3 %all-to-all-done = f32[16,1,6400]{2,1,0:T(1,128)S(1)} async-done(((f32[16,1,6400]{2,1,0:T(1,128)}), f32[16,1,6400]{2,1,0:T(1,128)S(1)}, u32[]{:S(2)}, u32[]{:S(2)}) %all-to-all-start) | async-done | bytes 409632 | tf_op jit(solution)/shard_map/all_to_all | solution.py:9
  45.2 5.6 %all-to-all-start.4 = ((bf16[16,2,2048]{2,1,0:T(2,128)(2,1)}), bf16[16,2,2048]{2,1,0:T(2,128)(2,1)S(1)}, u32[]{:S(2)}, u32[]{:S(2)}) async-start(bf16[16,2,2048]{2,1,0:T(2,128)(2,1)} %reshape.34), calls=%async_computation.4 | async-start | bytes 262144 | tf_op jit(solution)/shard_map/all_to_all | solution.py:9
  50.8 0.3 reduce_max.19
  51.1 0.0 copy-start.1
  51.1 4.6 %divide_convert_fusion = bf16[1,6400,256]{2,1,0:T(8,128)(2,1)S(1)} fusion(f32[1,6400,256]{2,1,0:T(8,128)} %param.3, f32[6400]{0:T(1024)S(1)} %reduce_max.19), kind=kLoop, calls=%fused_computation | loop fusion | flops 3276800 | bytes 9856000 | tf_op jit(solution)/shard_map/convert_element_type | solution.py:50
  55.7 0.0 copy-done.1
  55.8 1.4 fusion
  57.1 0.0 all-to-all-done.4
  57.1 0.0 copy-start
  57.1 0.7 copy-done
  57.8 48.2 %all_to_all.25 = bf16[16,1,200,256]{3,2,1,0:T(8,128)(2,1)S(1)} all-to-all(bf16[16,1,200,256]{3,2,1,0:T(8,128)(2,1)S(1)} %get-tuple-element.3), channel_id=1, replica_groups=mesh['expert'=16,'shard'=16] {'shard'}, dimensions={0} | all-to-all | bytes 3276800 | tf_op jit(solution)/shard_map/all_to_all | solution.py:40
  106.0 4.0 %all-to-all-start.2 = ((bf16[16,1,200,256]{3,2,1,0:T(8,128)(2,1)}), bf16[16,1,200,256]{3,2,1,0:T(8,128)(2,1)S(1)}, u32[]{:S(2)}, u32[]{:S(2)}) async-start(bf16[16,1,200,256]{3,2,1,0:T(8,128)(2,1)} %get-tuple-element.4), calls=%async_computation.2 | async-start | bytes 3276800 | tf_op jit(solution)/shard_map/all_to_all | solution.py:40
  110.0 1.4 reshape.35
  111.4 0.8 copy.21
  112.2 1.3 dynamic-slice.3
  113.5 40.1 %all-to-all-done.2 = bf16[16,1,200,256]{3,2,1,0:T(8,128)(2,1)S(1)} async-done(((bf16[16,1,200,256]{3,2,1,0:T(8,128)(2,1)}), bf16[16,1,200,256]{3,2,1,0:T(8,128)(2,1)S(1)}, u32[]{:S(2)}, u32[]{:S(2)}) %all-to-all-start.2) | async-done | bytes 1638432 | tf_op jit(solution)/shard_map/all_to_all | solution.py:40
  153.7 0.2 maximum_bitcast_fusion
  153.9 2.1 %copy.18 = bf16[16,1,50,8,256]{4,3,0,2,1:T(8,128)(2,1)} copy(bf16[16,1,50,8,256]{4,3,2,1,0:T(8,128)(2,1)S(1)} %maximum_bitcast_fusion) | data formatting | bytes 6553600 | tf_op jit(solution)/shard_map/reshape | solution.py:31
  (3 shorter events, 0.0 us)
Async XLA Ops:
  3.2 20.2 %all-to-all-start.3 = ((bf16[16,2,128]{2,1,0:T(2,128)(2,1)}), bf16[16,2,128]{2,1,0:T(2,128)(2,1)S(1)}, u32[]{:S(2)}, u32[]{:S(2)}) async-start(bf16[16,2,128]{2,1,0:T(2,128)(2,1)} %reshape.32), calls=%async_computation.3 | async-start | bytes 16384 | tf_op jit(solution)/shard_map/all_to_all | solution.py:9
  24.4 20.8 %all-to-all-start = ((f32[16,1,6400]{2,1,0:T(1,128)}), f32[16,1,6400]{2,1,0:T(1,128)S(1)}, u32[]{:S(2)}, u32[]{:S(2)}) async-start(f32[16,1,6400]{2,1,0:T(1,128)} %broadcast_in_dim.13), calls=%async_computation | async-start | bytes 819200 | tf_op jit(solution)/shard_map/all_to_all | solution.py:9
  45.2 11.9 %all-to-all-start.4 = ((bf16[16,2,2048]{2,1,0:T(2,128)(2,1)}), bf16[16,2,2048]{2,1,0:T(2,128)(2,1)S(1)}, u32[]{:S(2)}, u32[]{:S(2)}) async-start(bf16[16,2,2048]{2,1,0:T(2,128)(2,1)} %reshape.34), calls=%async_computation.4 | async-start | bytes 262144 | tf_op jit(solution)/shard_map/all_to_all | solution.py:9
  51.1 4.6 %copy-start.1 = (f32[6400]{0:T(1024)}, f32[6400]{0:T(1024)S(1)}, u32[]{:S(2)}) copy-start(f32[6400]{0:T(1024)S(1)} %reduce_max.19) | copy-start | bytes 76804
  57.1 0.7 copy-start
  106.0 47.7 %all-to-all-start.2 = ((bf16[16,1,200,256]{3,2,1,0:T(8,128)(2,1)}), bf16[16,1,200,256]{3,2,1,0:T(8,128)(2,1)S(1)}, u32[]{:S(2)}, u32[]{:S(2)}) async-start(bf16[16,1,200,256]{3,2,1,0:T(8,128)(2,1)} %get-tuple-element.4), calls=%async_computation.2 | async-start | bytes 3276800 | tf_op jit(solution)/shard_map/all_to_all | solution.py:40
where the time goes:
time: 157 us; the launch traced here: 156 us
  waiting for transfers between devices  60.1 us (38%)
  blocking collectives  48.2 us (31%)
  starting transfers between devices  24.6 us (16%)
  other arithmetic  11.7 us (7%)
  local copies, waits for them, and re-layouts  10.8 us (7%)
    all_to_all x1, blocking collectives, exchange_in_pieces(): lax.all_to_all(piece, axis, split_axis=0, concat_axis=0, tiled=True)  48.2 us
    all_to_all x1, waiting for transfers between devices, exchange_in_pieces(): lax.all_to_all(piece, axis, split_axis=0, concat_axis=0, tiled=True)  40.1 us
    all_to_all x3, starting transfers between devices, from_everyone(): return lax.all_to_all(copies, axis, split_axis=0, concat_axis=0, tiled=True)  20.6 us
    all_to_all x3, waiting for transfers between devices, from_everyone(): return lax.all_to_all(copies, axis, split_axis=0, concat_axis=0, tiled=True)  19.9 us
    convert_element_type x1, other arithmetic, per_device(): (train_down / jnp.expand_dims(scale_down, 2)).astype(jnp.bfloat16)  4.63 us
    unnamed x12, local copies, waits for them, and re-layouts  4.11 us
    all_to_all x1, starting transfers between devices, exchange_in_pieces(): lax.all_to_all(piece, axis, split_axis=0, concat_axis=0, tiled=True)  3.99 us
    reduce_max x1, other arithmetic, per_device(): scale_down = taken_together(jnp.max(jnp.abs(train_down), axis=2), 'shard')  3.78 us
  transfers between devices with their start and end apart: 4, of which 3 were waited for; matrix products, arithmetic and copies ran while one was open for 10% of the time, Pallas kernels for 0%

commit v1 on v0

v1 whole, which is shorter than its diff:
```python
import jax
import jax.numpy as jnp
from jax import lax
from jax.experimental import pallas as pl
from jax.experimental.pallas import tpu as pltpu
from jax.sharding import PartitionSpec as P

MESH = pl.DeviceIdType.MESH
PEERS = 16
ROWS, COLS = 400, 256
GROUPS = ROWS // 8
RAW = 16
EARLY = 64
FIRST = RAW + EARLY
REST = ROWS - FIRST
FAR = [(1, dy, dc) for dy in (2, 1, 3, 0) for dc in (0, 1)]
NEAR = [(0, dy, dc) for dy in (2, 1, 3, 0) for dc in (0, 1) if (dy, dc) != (0, 0)]
OFFSETS = FAR + NEAR
BACK = [OFFSETS.index((dz, -dy % 4, dc)) for dz, dy, dc in OFFSETS]


def kernel(
    x_ref, w_ref, g_ref, o_ref, sc_ref, rt_ref,
    xbuf, send, raw, early_mine, early_all, part_mine, part_all, full_all, wbuf, rb,
    load_sem, in_sem,
    early_s, early_r, part_s, part_r, raw_s, raw_r, full_s, full_r,
    da_s, da_r, db_s, db_r, z_s, z_r, xy_s, xy_r, co_s, co_r,
):
    e, s = lax.axis_index("expert"), lax.axis_index("shard")
    zl, xx = e // 4, e % 4
    zh, yy, cc = s // 8, (s // 2) % 4, s % 2
    zz = zh * 4 + zl

    def partner(k):
        dz, dy, dc = OFFSETS[k]
        return ((zh + dz) % 2) * 8 + ((yy + dy) % 4) * 2 + (cc + dc) % 2

    def on_line(k):
        z = (zz + k) % 8
        return {"expert": (z % 4) * 4 + xx, "shard": (z // 4) * 8 + yy * 2 + cc}

    def on_plane(k):
        x, y = (xx + k // 4) % 4, (yy + k % 4) % 4
        return {"expert": zl * 4 + x, "shard": zh * 8 + y * 2 + cc}

    order = [partner(k) for k in range(PEERS - 1)] + [s]
    loads = []
    for k, d in enumerate(order):
        c = pltpu.make_async_copy(x_ref.at[pl.ds(d * ROWS, ROWS)], xbuf.at[d], load_sem.at[k])
        c.start()
        loads.append(c)
    small = [
        pltpu.make_async_copy(w_ref, wbuf.at[0], in_sem.at[0]),
        pltpu.make_async_copy(g_ref, wbuf.at[1], in_sem.at[1]),
    ]
    for c in small:
        c.start()

    barrier = pltpu.get_barrier_semaphore()
    greeted = 0
    for k in range(PEERS - 1):
        pl.semaphore_signal(barrier, inc=1, device_id={"shard": partner(k)}, device_id_type=MESH)
        greeted += 1
    for k in range(1, 8):
        if k != 4:
            pl.semaphore_signal(barrier, inc=1, device_id=on_line(k), device_id_type=MESH)
            greeted += 1
    for k in range(1, 16):
        if k // 4:
            pl.semaphore_signal(barrier, inc=1, device_id=on_plane(k), device_id_type=MESH)
            greeted += 1

    for c in small:
        c.wait()
    rb[xx, yy, cc, zz] = (wbuf[0] * wbuf[1]).astype(jnp.bfloat16).astype(jnp.float32)

    lane = lax.broadcasted_iota(jnp.int32, (8, 128), 1)
    for c in loads:
        c.wait()

    def maxima(d, early):
        part = jnp.zeros((8, 128), jnp.float32)
        for g in range(GROUPS):
            v = jnp.abs(xbuf[d, 8 * g : 8 * g + 8, :])
            top = jnp.max(jnp.maximum(v[:, :128], v[:, 128:]), axis=1, keepdims=True)
            part = jnp.where(lane == g, top, part)
            if RAW <= 8 * g < FIRST:
                early = jnp.where(lane == d * (EARLY // 8) + g - RAW // 8, top, early)
        part_mine[d] = part
        return early

    early_mine[...] = lax.fori_loop(0, PEERS, maxima, jnp.zeros((8, 128), jnp.float32))
    early_all[s] = early_mine[...]
    part_all[s] = part_mine[s]

    pl.semaphore_wait(barrier, greeted)

    def remote(src, dst, ss, rs, device):
        c = pltpu.make_async_remote_copy(
            src_ref=src, dst_ref=dst, send_sem=ss, recv_sem=rs, device_id=device, device_id_type=MESH
        )
        c.start()
        return c

    pending = []
    early, part, rawc, full, da, db = [], [], [], [], [], []
    for k in range(PEERS - 1):
        early.append(remote(early_mine, early_all.at[s], early_s.at[k], early_r.at[k], {"shard": partner(k)}))
    for k in range(PEERS - 1):
        d = partner(k)
        part.append(remote(part_mine.at[d], part_all.at[s], part_s.at[k], part_r.at[k], {"shard": d}))
    line = [
        remote(rb.at[xx, yy, cc, zz], rb.at[xx, yy, cc, zz], z_s.at[k], z_r.at[k], on_line(k)) for k in range(1, 8)
    ]
    for k in range(PEERS - 1):
        d = partner(k)
        rawc.append(remote(xbuf.at[d, pl.ds(0, RAW)], raw.at[s], raw_s.at[k], raw_r.at[k], {"shard": d}))

    for c in part:
        c.wait_recv()
    mine = jnp.max(part_all[...], axis=0)
    full_all[s] = mine
    for c in early:
        c.wait_recv()
    inverse_early = 1.0 / jnp.max(early_all[...], axis=0)
    for k in range(PEERS - 1):
        full.append(remote(full_all.at[s], full_all.at[s], full_s.at[k], full_r.at[k], {"shard": partner(k)}))

    mine_safe = jnp.where(lane < GROUPS, mine, 1.0)
    inverse_mine = 1.0 / mine_safe

    def early_rows(d):
        for j in range(EARLY // 16):
            tops = []
            for h in range(2):
                at = d * (EARLY // 8) + 2 * j + h
                tops.append(jnp.sum(jnp.where(lane == at, inverse_early, 0.0), axis=1, keepdims=True))
            lo = RAW + 16 * j
            send[d, lo : lo + 16, :] = (xbuf[d, lo : lo + 16, :] * jnp.concatenate(tops, axis=0)).astype(jnp.bfloat16)

    columns = pl.ds(pl.multiple_of(s * COLS, COLS), COLS)

    def send_early(k):
        d = partner(k)
        da.append(
            remote(
                send.at[d, pl.ds(RAW, EARLY)], o_ref.at[pl.ds(RAW, EARLY), columns],
                da_s.at[k], da_r.at[k], {"shard": d},
            )
        )

    for k in range(PEERS - 1):
        early_rows(partner(k))
        if k:
            send_early(k - 1)
    send_early(PEERS - 2)

    def rest_rows(d):
        inverse = 1.0 / jnp.where(lane < GROUPS, full_all[d], 1.0)
        for j in range(FIRST // 16, ROWS // 16):
            tops = jnp.concatenate([inverse[:, 2 * j : 2 * j + 1], inverse[:, 2 * j + 1 : 2 * j + 2]], axis=0)
            send[d, 16 * j : 16 * j + 16, :] = (xbuf[d, 16 * j : 16 * j + 16, :] * tops).astype(jnp.bfloat16)

    def send_rest(k):
        d = partner(k)
        db.append(
            remote(
                send.at[d, pl.ds(FIRST, REST)], o_ref.at[pl.ds(FIRST, REST), columns],
                db_s.at[k], db_r.at[k], {"shard": d},
            )
        )

    for k in range(PEERS - 1):
        full[BACK[k]].wait_recv()
        rest_rows(partner(k))
        if k:
            send_rest(k - 1)
    send_rest(PEERS - 2)

    for c in line:
        c.wait_recv()
    plane = [
        remote(rb.at[xx, yy, cc], rb.at[xx, yy, cc], xy_s.at[k], xy_r.at[k], on_plane(k)) for k in range(1, 16)
    ]

    for j in range(ROWS // 16):
        tops = jnp.concatenate([inverse_mine[:, 2 * j : 2 * j + 1], inverse_mine[:, 2 * j + 1 : 2 * j + 2]], axis=0)
        o_ref[16 * j : 16 * j + 16, columns] = (xbuf[s, 16 * j : 16 * j + 16, :] * tops).astype(jnp.bfloat16)
    for c in rawc:
        c.wait_recv()
    for k in range(PEERS - 1):
        d = partner(k)
        for j in range(RAW // 16):
            tops = jnp.concatenate([inverse_mine[:, 2 * j : 2 * j + 1], inverse_mine[:, 2 * j + 1 : 2 * j + 2]], axis=0)
            o_ref[16 * j : 16 * j + 16, pl.ds(pl.multiple_of(d * COLS, COLS), COLS)] = (
                raw[d, 16 * j : 16 * j + 16, :] * tops
            ).astype(jnp.bfloat16)

    sub = lax.broadcasted_iota(jnp.int32, (8, 128), 0)
    for b in range(pl.cdiv(ROWS, 128)):
        row = jnp.zeros((8, 128), jnp.float32)
        for g in range(16 * b, min(16 * b + 16, GROUPS)):
            here = (lane // 8 == g - 16 * b) & (sub == lane % 8)
            row = jnp.where(here, jnp.broadcast_to(mine[:, g : g + 1], (8, 128)), row)
        width = min(128, ROWS - 128 * b)
        sc_ref[:, 128 * b : 128 * b + width] = jnp.max(row, axis=0, keepdims=True)[:, :width]

    for c in plane:
        c.wait_recv()
    other = remote(
        rb.at[:, :, cc], rb.at[:, :, cc], co_s.at[0], co_r.at[0],
        {"shard": zh * 8 + yy * 2 + 1 - cc},
    )
    other.wait_recv()

    def router_columns(t, carry):
        h, y, c = t // 8, (t // 2) % 4, t % 2
        rows = [rb[r % 4, y, c, h * 4 + r // 4] for r in range(16)]
        rt_ref[:, pl.ds(pl.multiple_of(t * COLS, COLS), COLS)] = jnp.concatenate(rows, axis=0).astype(jnp.bfloat16)
        return carry

    lax.fori_loop(0, PEERS, router_columns, 0)

    for c in da + db:
        c.wait_recv()
    for c in early + part + line + rawc + full + da + db + plane + [other]:
        c.wait_send()


def per_device(train_down, router_weight, router_gain):
    x = train_down[0]
    w = router_weight.reshape(1, COLS)
    g = router_gain.reshape(1, COLS)
    f32, bf16 = jnp.float32, jnp.bfloat16
    dma = pltpu.SemaphoreType.DMA
    pairs = lambda n: [dma((n,)), dma((n,))]
    n = PEERS - 1
    hbm = pl.BlockSpec(memory_space=pltpu.HBM)
    vmem = pl.BlockSpec(memory_space=pltpu.VMEM)
    o, sc, rt = pl.pallas_call(
        kernel,
        out_shape=(
            pltpu.VMEM((ROWS, PEERS * COLS), bf16),
            pltpu.VMEM((1, ROWS), f32),
            pltpu.VMEM((PEERS, PEERS * COLS), bf16),
        ),
        in_specs=[hbm] * 3,
        out_specs=(vmem,) * 3,
        scratch_shapes=[
            pltpu.VMEM((PEERS, ROWS, COLS), f32),
            pltpu.VMEM((PEERS, ROWS, COLS), bf16),
            pltpu.VMEM((PEERS, RAW, COLS), f32),
            pltpu.VMEM((8, 128), f32),
            pltpu.VMEM((PEERS, 8, 128), f32),
            pltpu.VMEM((PEERS, 8, 128), f32),
            pltpu.VMEM((PEERS, 8, 128), f32),
            pltpu.VMEM((PEERS, 8, 128), f32),
            pltpu.VMEM((2, 1, COLS), f32),
            pltpu.VMEM((4, 4, 2, 8, 1, COLS), f32),
            dma((PEERS,)), dma((2,)),
            *pairs(n), *pairs(n), *pairs(n), *pairs(n), *pairs(n), *pairs(n),
            *pairs(8), *pairs(16), *pairs(1),
        ],
        compiler_params=pltpu.CompilerParams(
            collective_id=0, has_side_effects=True, vmem_limit_bytes=40 * 2**20
        ),
        name="exchange",
    )(x, w, g)
    return o[None], sc, rt.T


def solution(mesh):
    in_specs = (P("expert", None, "shard"), P("shard", "expert"), P("shard"))
    out_specs = (P("expert", "shard", None), P("expert", "shard"), P())
    return jax.shard_map(per_device, mesh=mesh, in_specs=in_specs, out_specs=out_specs, check_vma=False)
```

time: 157 us -> 106 us (0.68)
  the two profiles are of different devices: /device:TPU:35 before, /device:TPU:1 now
where the time goes in v1:
time: 106 us
  Pallas kernels  98.3 us (93%)
  local copies, waits for them, and re-layouts  7.15 us (7%)
    pallas_call x1, Pallas kernels, per_device(): pl.pallas_call(kernel, out_shape=(pltpu.VMEM((ROWS, PEERS * COLS), bf16),...  98.3 us
    unnamed x9, local copies, waits for them, and re-layouts  7.15 us

profile of v1, /device:TPU:1, one launch (start us, length us, event | category | flops | bytes accessed | tf_op | source)
XLA Modules:
  0.0 106.1 jit_solution(2361404831728913617)
XLA Ops:
  0.6 0.0 copy-start
  0.6 2.9 %copy-done = f32[1,6400,256]{2,1,0:T(8,128)S(1)} copy-done((f32[1,6400,256]{2,1,0:T(8,128)S(1)}, f32[1,6400,256]{2,1,0:T(8,128)}, u32[]{:S(2)}) %copy-start) | copy-done | bytes 6553624
  3.5 0.0 copy-start.1
  3.5 0.7 copy-done.1
  4.2 0.0 copy-start.2
  4.2 0.7 copy-done.2
  4.8 98.3 %exchange.1 = (bf16[400,4096]{1,0:T(8,128)(2,1)S(1)}, f32[1,400]{1,0:T(1,128)S(1)}, bf16[16,4096]{1,0:T(8,128)(2,1)S(1)}) custom-call(f32[6400,256]{1,0:T(8,128)S(1)} %bitcast.7, f32[1,256]{1,0:T(1,128)S(1)} %bitcast.8, f32[1,256]{1,0:T(1,128)S(1)} %bitcast.9), custom_call_target="tpu_custom_call" | custom-call | tf_op jit(solution)/shard_map/exchange/pallas_call | solution.py:240
  103.2 1.7 %copy.9 = bf16[1,400,4096]{2,1,0:T(8,128)(2,1)} copy(bf16[1,400,4096]{2,1,0:T(8,128)(2,1)S(1)} %bitcast.5) | data formatting | bytes 6553600
  104.9 0.6 copy.10
  105.4 0.7 copy.11
Async XLA Ops:
  0.6 2.9 %copy-start = (f32[1,6400,256]{2,1,0:T(8,128)S(1)}, f32[1,6400,256]{2,1,0:T(8,128)}, u32[]{:S(2)}) copy-start(f32[1,6400,256]{2,1,0:T(8,128)} %param.3) | copy-start | bytes 19660804
  3.5 0.7 copy-start.1
  4.2 0.7 copy-start.2

commit v2 on v1

v2 whole, which is shorter than its diff:
```python
import jax
import jax.numpy as jnp
from jax import lax
from jax.experimental import pallas as pl
from jax.experimental.pallas import tpu as pltpu
from jax.sharding import PartitionSpec as P

MESH = pl.DeviceIdType.MESH
PEERS = 16
HALF = 8
ROWS, COLS = 400, 256
GROUPS = ROWS // 8
RAW = 16
EARLY = 64
FIRST = RAW + EARLY
REST = ROWS - FIRST
FAR = [(1, dy, dc) for dy in (2, 1, 3, 0) for dc in (0, 1)]
NEAR = [(0, dy, dc) for dy in (2, 1, 3, 0) for dc in (0, 1) if (dy, dc) != (0, 0)]
OFFSETS = FAR + NEAR
BACK = [OFFSETS.index((dz, -dy % 4, dc)) for dz, dy, dc in OFFSETS]


def kernel(
    x_ref, w_ref, g_ref, o_ref, sc_ref, rt_ref,
    xbuf, send, raw, early_mine, early_all, early_out, early_in, part_mine, part_all, half_out, half_in, full_all,
    wbuf, rb,
    load_sem, in_sem, here_sem,
    early_s, early_r, part_s, part_r, ez_s, ez_r, hz_s, hz_r, full_s, full_r,
    raw_s, raw_r, da_s, da_r, db_s, db_r, z_s, z_r, xy_s, xy_r, co_s, co_r,
):
    e, s = lax.axis_index("expert"), lax.axis_index("shard")
    zl, xx = e // 4, e % 4
    zh, yy, cc = s // 8, (s // 2) % 4, s % 2
    zz = zh * 4 + zl
    u = s % 8

    def partner(k):
        dz, dy, dc = OFFSETS[k]
        return ((zh + dz) % 2) * 8 + ((yy + dy) % 4) * 2 + (cc + dc) % 2

    def on_line(k):
        z = (zz + k) % 8
        return {"expert": (z % 4) * 4 + xx, "shard": (z // 4) * 8 + yy * 2 + cc}

    def on_plane(k):
        x, y = (xx + k // 4) % 4, (yy + k % 4) % 4
        return {"expert": zl * 4 + x, "shard": zh * 8 + y * 2 + cc}

    near = range(len(FAR), PEERS - 1)
    across = {"shard": (s + 8) % 16}

    barrier = pltpu.get_barrier_semaphore()
    greeted = [on_line(k) for k in (4, 3, 5, 2, 6, 1, 7)]
    greeted += [on_plane(k) for k in range(4, 16)]
    greeted += [{"shard": partner(k)} for k in near]
    for device in greeted:
        pl.semaphore_signal(barrier, inc=1, device_id=device, device_id_type=MESH)

    def load(d):
        return pltpu.make_async_copy(x_ref.at[pl.ds(d * ROWS, ROWS)], xbuf.at[d], load_sem.at[d])

    def start_load(d, carry):
        load(d).start()
        return carry

    lax.fori_loop(0, PEERS, start_load, 0)
    small = [
        pltpu.make_async_copy(w_ref, wbuf.at[0], in_sem.at[0]),
        pltpu.make_async_copy(g_ref, wbuf.at[1], in_sem.at[1]),
    ]
    for c in small:
        c.start()
    for c in small:
        c.wait()
    rb[xx, yy, cc, zz] = (wbuf[0] * wbuf[1]).astype(jnp.bfloat16).astype(jnp.float32)

    lane = lax.broadcasted_iota(jnp.int32, (8, 128), 1)

    def maxima(v, early):
        part = jnp.zeros((8, 128), jnp.float32)
        for h in range(2):
            d = h * HALF + v
            load(d).wait()
            for g in range(GROUPS):
                a = jnp.abs(xbuf[d, 8 * g : 8 * g + 8, :])
                top = jnp.max(jnp.maximum(a[:, :128], a[:, 128:]), axis=1, keepdims=True)
                part = jnp.where(lane == h * 64 + g, top, part)
                if RAW <= 8 * g < FIRST:
                    early = jnp.where(lane == d * (EARLY // 8) + g - RAW // 8, top, early)
        part_mine[v] = part
        return early

    early_mine[...] = lax.fori_loop(0, HALF, maxima, jnp.zeros((8, 128), jnp.float32))
    early_all[u] = early_mine[...]
    part_all[u] = part_mine[u]

    pl.semaphore_wait(barrier, len(greeted))

    started, arrived = [], set()

    def remote(src, dst, ss, rs, device):
        c = pltpu.make_async_remote_copy(
            src_ref=src, dst_ref=dst, send_sem=ss, recv_sem=rs, device_id=device, device_id_type=MESH
        )
        c.start()
        started.append(c)
        return c

    def arrive(copies):
        for c in copies:
            c.wait_recv()
            arrived.add(id(c))

    def drain():
        for c in started:
            if id(c) not in arrived:
                c.wait_recv()
            c.wait_send()

    for k in near:
        pl.semaphore_signal(here_sem, inc=1, device_id={"shard": partner(k)}, device_id_type=MESH)
    early = [
        remote(early_mine, early_all.at[u], early_s.at[i], early_r.at[i], {"shard": partner(k)})
        for i, k in enumerate(near)
    ]
    part = [
        remote(part_mine.at[partner(k) % 8], part_all.at[u], part_s.at[i], part_r.at[i], {"shard": partner(k)})
        for i, k in enumerate(near)
    ]
    line = [
        remote(rb.at[xx, yy, cc, zz], rb.at[xx, yy, cc, zz], z_s.at[k], z_r.at[k], on_line(k)) for k in range(1, 8)
    ]
    pl.semaphore_wait(here_sem, len(near))
    rawc = []
    for k in range(PEERS - 1):
        d = partner(k)
        rawc.append(remote(xbuf.at[d, pl.ds(0, RAW)], raw.at[s], raw_s.at[k], raw_r.at[k], {"shard": d}))

    arrive(early)
    early_out[...] = jnp.max(early_all[...], axis=0)
    arrive(part)
    half_out[...] = jnp.max(part_all[...], axis=0)
    ez = remote(early_out, early_in, ez_s.at[0], ez_r.at[0], across)
    hz = remote(half_out, half_in, hz_s.at[0], hz_r.at[0], across)
    arrive([ez])
    inverse_early = 1.0 / jnp.maximum(early_out[...], early_in[...])
    arrive([hz])
    full_all[u] = jnp.maximum(half_out[...], half_in[...])
    full = [
        remote(full_all.at[u], full_all.at[u], full_s.at[i], full_r.at[i], {"shard": partner(k)})
        for i, k in enumerate(near)
    ]

    def early_rows(d):
        for j in range(EARLY // 16):
            tops = []
            for h in range(2):
                at = d * (EARLY // 8) + 2 * j + h
                tops.append(jnp.sum(jnp.where(lane == at, inverse_early, 0.0), axis=1, keepdims=True))
            lo = RAW + 16 * j
            send[d, lo : lo + 16, :] = (xbuf[d, lo : lo + 16, :] * jnp.concatenate(tops, axis=0)).astype(jnp.bfloat16)

    columns = pl.ds(pl.multiple_of(s * COLS, COLS), COLS)

    def send_rows(lo, count, ss, rs, k):
        d = partner(k)
        return remote(
            send.at[d, pl.ds(lo, count)], o_ref.at[pl.ds(lo, count), columns], ss.at[k], rs.at[k], {"shard": d}
        )

    for k in range(PEERS - 1):
        early_rows(partner(k))
        if k:
            send_rows(RAW, EARLY, da_s, da_r, k - 1)
    send_rows(RAW, EARLY, da_s, da_r, PEERS - 2)


    def inverse_of(h, tile):
        tile = jnp.where(lane % 64 < GROUPS, tile, 1.0)
        tile = 1.0 / tile
        return jnp.where(h == 0, tile, pltpu.roll(tile, 64, 1))

    def tops_of(inverse, j):
        return jnp.concatenate([inverse[:, 2 * j : 2 * j + 1], inverse[:, 2 * j + 1 : 2 * j + 2]], axis=0)

    def rest_rows(d):
        inverse = inverse_of(d // 8, full_all[d % 8])
        for j in range(FIRST // 16, ROWS // 16):
            send[d, 16 * j : 16 * j + 16, :] = (xbuf[d, 16 * j : 16 * j + 16, :] * tops_of(inverse, j)).astype(
                jnp.bfloat16
            )

    arrive(full)
    for k in range(PEERS - 1):
        rest_rows(partner(k))
        if k:
            send_rows(FIRST, REST, db_s, db_r, k - 1)
    send_rows(FIRST, REST, db_s, db_r, PEERS - 2)

    arrive(line)
    plane = [
        remote(rb.at[xx, yy, cc], rb.at[xx, yy, cc], xy_s.at[k], xy_r.at[k], on_plane(k)) for k in range(1, 16)
    ]

    mine = full_all[u]
    inverse_mine = inverse_of(zh, mine)
    for j in range(ROWS // 16):
        o_ref[16 * j : 16 * j + 16, columns] = (xbuf[s, 16 * j : 16 * j + 16, :] * tops_of(inverse_mine, j)).astype(
            jnp.bfloat16
        )
    arrive(rawc)
    for k in range(PEERS - 1):
        d = partner(k)
        for j in range(RAW // 16):
            o_ref[16 * j : 16 * j + 16, pl.ds(pl.multiple_of(d * COLS, COLS), COLS)] = (
                raw[d, 16 * j : 16 * j + 16, :] * tops_of(inverse_mine, j)
            ).astype(jnp.bfloat16)

    mine = jnp.where(zh == 0, mine, pltpu.roll(mine, 64, 1))
    sub = lax.broadcasted_iota(jnp.int32, (8, 128), 0)
    for b in range(pl.cdiv(ROWS, 128)):
        row = jnp.zeros((8, 128), jnp.float32)
        for g in range(16 * b, min(16 * b + 16, GROUPS)):
            here = (lane // 8 == g - 16 * b) & (sub == lane % 8)
            row = jnp.where(here, jnp.broadcast_to(mine[:, g : g + 1], (8, 128)), row)
        width = min(128, ROWS - 128 * b)
        sc_ref[:, 128 * b : 128 * b + width] = jnp.max(row, axis=0, keepdims=True)[:, :width]

    arrive(plane)
    other = remote(
        rb.at[:, :, cc], rb.at[:, :, cc], co_s.at[0], co_r.at[0],
        {"shard": zh * 8 + yy * 2 + 1 - cc},
    )
    arrive([other])

    def router_columns(t, carry):
        h, y, c = t // 8, (t // 2) % 4, t % 2
        rows = [rb[r % 4, y, c, h * 4 + r // 4] for r in range(16)]
        rt_ref[:, pl.ds(pl.multiple_of(t * COLS, COLS), COLS)] = jnp.concatenate(rows, axis=0).astype(jnp.bfloat16)
        return carry

    lax.fori_loop(0, PEERS, router_columns, 0)

    drain()


def finish(o_ref, sc_ref, rt_ref, out_o, out_sc, out_rt, sem):
    copies = [
        pltpu.make_async_copy(o_ref, out_o, sem.at[0]),
        pltpu.make_async_copy(sc_ref, out_sc, sem.at[1]),
        pltpu.make_async_copy(rt_ref, out_rt, sem.at[2]),
    ]
    for c in copies:
        c.start()
    for c in copies:
        c.wait()


def per_device(train_down, router_weight, router_gain):
    keep = lambda a: pltpu.with_memory_space_constraint(a, pltpu.HBM)
    x = keep(train_down[0])
    w = keep(router_weight.reshape(1, COLS))
    g = keep(router_gain.reshape(1, COLS))
    f32, bf16 = jnp.float32, jnp.bfloat16
    dma = pltpu.SemaphoreType.DMA
    pairs = lambda n: [dma((n,)), dma((n,))]
    tile = lambda *n: pltpu.VMEM((*n, 8, 128), f32)
    n, m = PEERS - 1, HALF - 1
    hbm = pl.BlockSpec(memory_space=pltpu.HBM)
    vmem = pl.BlockSpec(memory_space=pltpu.VMEM)
    o, sc, rt = pl.pallas_call(
        kernel,
        out_shape=(
            pltpu.VMEM((ROWS, PEERS * COLS), bf16),
            pltpu.VMEM((1, ROWS), f32),
            pltpu.VMEM((PEERS, PEERS * COLS), bf16),
        ),
        in_specs=[hbm] * 3,
        out_specs=(vmem,) * 3,
        scratch_shapes=[
            pltpu.VMEM((PEERS, ROWS, COLS), f32),
            pltpu.VMEM((PEERS, ROWS, COLS), bf16),
            pltpu.VMEM((PEERS, RAW, COLS), f32),
            tile(), tile(HALF), tile(), tile(),
            tile(HALF), tile(HALF), tile(), tile(), tile(HALF),
            pltpu.VMEM((2, 1, COLS), f32),
            pltpu.VMEM((4, 4, 2, 8, 1, COLS), f32),
            dma((PEERS,)), dma((2,)), pltpu.SemaphoreType.REGULAR,
            *pairs(m), *pairs(m), *pairs(1), *pairs(1), *pairs(m),
            *pairs(n), *pairs(n), *pairs(n),
            *pairs(8), *pairs(16), *pairs(1),
        ],
        compiler_params=pltpu.CompilerParams(
            collective_id=0, has_side_effects=True, vmem_limit_bytes=40 * 2**20
        ),
        name="exchange",
    )(x, w, g)
    inside = lambda a: pltpu.with_memory_space_constraint(a, pltpu.VMEM)
    ready, scale, router = pl.pallas_call(
        finish,
        out_shape=(
            jax.ShapeDtypeStruct((ROWS, PEERS * COLS), bf16),
            jax.ShapeDtypeStruct((1, ROWS), f32),
            jax.ShapeDtypeStruct((PEERS, PEERS * COLS), bf16),
        ),
        in_specs=[vmem] * 3,
        out_specs=(hbm,) * 3,
        scratch_shapes=[dma((3,))],
        name="finish",
    )(inside(o), inside(sc), inside(rt))
    return ready[None], scale, router.T


def solution(mesh):
    in_specs = (P("expert", None, "shard"), P("shard", "expert"), P("shard"))
    out_specs = (P("expert", "shard", None), P("expert", "shard"), P())
    return jax.shard_map(per_device, mesh=mesh, in_specs=in_specs, out_specs=out_specs, check_vma=False)
```

time: 106 us -> 95.1 us (0.90)
  the two profiles are of different devices: /device:TPU:1 before, /device:TPU:35 now
where the time goes in v2:
time: 95.1 us; the launch traced here: 94.1 us
  Pallas kernels  93.5 us (98%)
    pallas_call x1, Pallas kernels, per_device(): pl.pallas_call(kernel, out_shape=(pltpu.VMEM((ROWS, PEERS * COLS), bf16),...  91.7 us

profile of v2, /device:TPU:35, one launch (start us, length us, event | category | flops | bytes accessed | tf_op | source)
XLA Modules:
  0.0 94.1 jit_solution(7482008397762836283)
XLA Ops:
  0.6 91.7 %exchange.1 = (bf16[400,4096]{1,0:T(8,128)(2,1)S(1)}, f32[1,400]{1,0:T(1,128)S(1)}, bf16[16,4096]{1,0:T(8,128)(2,1)S(1)}) custom-call(f32[6400,256]{1,0:T(8,128)} %bitcast.5, f32[1,256]{1,0:T(1,128)} %bitcast.6, f32[1,256]{1,0:T(1,128)} %bitcast.7), custom_call_target="tpu_custom_call" | custom-call | tf_op jit(solution)/shard_map/exchange/pallas_call | solution.py:271
  92.4 1.8 %finish.1 = (bf16[400,4096]{1,0:T(8,128)(2,1)}, f32[1,400]{1,0:T(1,128)}, bf16[16,4096]{1,0:T(8,128)(2,1)}) custom-call(bf16[400,4096]{1,0:T(8,128)(2,1)S(1)} %get-tuple-element.9.o_ref, f32[1,400]{1,0:T(1,128)S(1)} %get-tuple-element.10.sc_ref, bf16[16,4096]{1,0:T(8,128)(2,1)S(1)} %get-tuple-element.11.rt_ref), custom_call_target="tpu_custom_call" | custom-call | tf_op jit(solution)/shard_map/finish/pallas_call | solution.py:299

commit v3 on v2

v3 whole, which is shorter than its diff:
```python
import jax
import jax.numpy as jnp
from jax import lax
from jax.experimental import pallas as pl
from jax.experimental.pallas import tpu as pltpu
from jax.sharding import PartitionSpec as P

MESH = pl.DeviceIdType.MESH
PEERS = 16
HALF = 8
ROWS, COLS = 400, 256
GROUPS = ROWS // 8
BLOCK = 64
STEPS = 2
EARLY = BLOCK * STEPS
REST = ROWS - EARLY
CUTS = 5
LOAD = 4
PART, HZ, FULL, DATA_REST, LINE, PLANE, OTHER = range(7)
EARLIES = range(7, 7 + STEPS)
DATA_EARLY = range(7 + STEPS, 7 + 2 * STEPS)
KINDS = 7 + 2 * STEPS
FAR = [(1, dy, dc) for dy in (2, 1, 3, 0) for dc in (0, 1)]
NEAR = [(0, dy, dc) for dy in (2, 1, 3, 0) for dc in (0, 1) if (dy, dc) != (0, 0)]
OFFSETS = FAR + NEAR


def kernel(
    x_ref, w_ref, g_ref, o_ref, sc_ref, rt_ref,
    xbuf, send, early_mine, early_all, part_mine, part_all, half_out, half_in, full_all,
    wbuf, rb,
    load_sem, in_sem, sent, got,
):
    e, s = lax.axis_index("expert"), lax.axis_index("shard")
    zl, xx = e // 4, e % 4
    zh, yy, cc = s // 8, (s // 2) % 4, s % 2
    zz = zh * 4 + zl
    u = s % 8

    def partner(k):
        dz, dy, dc = OFFSETS[k]
        return ((zh + dz) % 2) * 8 + ((yy + dy) % 4) * 2 + (cc + dc) % 2

    def on_line(k):
        z = (zz + k) % 8
        return {"expert": (z % 4) * 4 + xx, "shard": (z // 4) * 8 + yy * 2 + cc}

    def on_plane(k):
        x, y = (xx + k // 4) % 4, (yy + k % 4) % 4
        return {"expert": zl * 4 + x, "shard": zh * 8 + y * 2 + cc}

    near = range(len(FAR), PEERS - 1)
    across = {"shard": (s + 8) % 16}

    barrier = pltpu.get_barrier_semaphore()
    greeted = [{"shard": partner(k)} for k in range(PEERS - 1)]
    greeted += [on_line(k) for k in (3, 5, 2, 6, 1, 7)]
    greeted += [on_plane(k) for k in range(4, 16)]
    for device in greeted:
        pl.semaphore_signal(barrier, inc=1, device_id=device, device_id_type=MESH)

    def load(q):
        if q < STEPS:
            here = (slice(None), pl.ds(q * BLOCK, BLOCK))
        else:
            here = (pl.ds((q - STEPS) * LOAD, LOAD), pl.ds(EARLY, REST))
        return pltpu.make_async_copy(x_ref.at[here], xbuf.at[here], load_sem.at[q])

    loads = [load(q) for q in range(STEPS + PEERS // LOAD)]
    for c in loads:
        c.start()
    pltpu.make_async_copy(w_ref, wbuf.at[0], in_sem).start()
    pltpu.make_async_copy(g_ref, wbuf.at[1], in_sem).start()

    lane = lax.broadcasted_iota(jnp.int32, (8, 128), 1)

    def top_of(d, g):
        a = jnp.abs(xbuf[d, 8 * g : 8 * g + 8, :])
        return jnp.max(jnp.maximum(a[:, :128], a[:, 128:]), axis=1, keepdims=True)

    def early_maxima(t):
        def one(d, early):
            h, v = d // HALF, d % HALF
            part = part_mine[v]
            for g in range(BLOCK // 8):
                top = top_of(d, t * (BLOCK // 8) + g)
                part = jnp.where(lane == h * 64 + t * (BLOCK // 8) + g, top, part)
                early = jnp.where(lane == d * (BLOCK // 8) + g, top, early)
            part_mine[v] = part
            return early

        loads[t].wait()
        early_mine[t] = lax.fori_loop(0, PEERS, one, jnp.zeros((8, 128), jnp.float32))
        early_all[t, s] = early_mine[t]

    def rest_maxima(d, carry):
        h, v = d // HALF, d % HALF
        part = part_mine[v]
        for g in range(EARLY // 8, GROUPS):
            part = jnp.where(lane == h * 64 + g, top_of(d, g), part)
        part_mine[v] = part
        return carry

    part_mine[...] = jnp.zeros((HALF, 8, 128), jnp.float32)
    early_maxima(0)

    pl.semaphore_wait(barrier, len(greeted))

    def remote(src, dst, kind, device):
        pltpu.make_async_remote_copy(
            src_ref=src, dst_ref=dst, send_sem=sent.at[kind], recv_sem=got.at[kind],
            device_id=device, device_id_type=MESH,
        ).start()

    amount = {
        PART: part_all.at[pl.ds(0, HALF - 1)],
        HZ: half_in,
        FULL: full_all.at[pl.ds(0, HALF - 1)],
        DATA_REST: send.at[pl.ds(0, PEERS - 1), pl.ds(0, REST)],
        LINE: rb.at[0, 0, 0, pl.ds(0, 7)],
        PLANE: xbuf.at[0, pl.ds(0, 15 * 8)],
        OTHER: xbuf.at[0, pl.ds(0, 16 * 8)],
    }

    for t in range(STEPS):
        amount[EARLIES[t]] = early_all.at[t, pl.ds(0, PEERS - 1)]
        amount[DATA_EARLY[t]] = send.at[pl.ds(0, PEERS - 1), pl.ds(0, BLOCK)]

    def arrive(kind):
        pltpu.make_async_copy(amount[kind], amount[kind], got.at[kind]).wait()

    def leave(kind):
        pltpu.make_async_copy(amount[kind], amount[kind], sent.at[kind]).wait()

    for t in range(STEPS):
        if t:
            early_maxima(t)
        for k in range(PEERS - 1):
            remote(early_mine.at[t], early_all.at[t, s], EARLIES[t], {"shard": partner(k)})

    for q in range(PEERS // LOAD):
        loads[STEPS + q].wait()
        lax.fori_loop(q * LOAD, q * LOAD + LOAD, rest_maxima, 0)
    part_all[u] = part_mine[u]
    for k in near:
        remote(part_mine.at[partner(k) % 8], part_all.at[u], PART, {"shard": partner(k)})
    pltpu.make_async_copy(wbuf, wbuf, in_sem).wait()
    rb[xx, yy, cc, zz] = (wbuf[0] * wbuf[1]).astype(jnp.bfloat16).astype(jnp.float32)
    for k in range(1, 8):
        remote(rb.at[xx, yy, cc, zz], rb.at[xx, yy, cc, zz], LINE, on_line(k))

    def early_rows(t, d, inverse):
        for j in range(BLOCK // 16):
            tops = []
            for h in range(2):
                at = d * (BLOCK // 8) + 2 * j + h
                tops.append(jnp.sum(jnp.where(lane == at, inverse, 0.0), axis=1, keepdims=True))
            lo = t * BLOCK + 16 * j
            send[d, lo : lo + 16, :] = (xbuf[d, lo : lo + 16, :] * jnp.concatenate(tops, axis=0)).astype(jnp.bfloat16)

    columns = pl.ds(pl.multiple_of(s * COLS, COLS), COLS)

    def send_rows(lo, count, kind, k):
        d = partner(k)
        remote(send.at[d, pl.ds(lo, count)], o_ref.at[pl.ds(lo, count), columns], kind, {"shard": d})

    for t in range(STEPS):
        arrive(EARLIES[t])
        if t == 0:
            arrive(PART)
            half_out[...] = jnp.max(part_all[...], axis=0)
            remote(half_out, half_in, HZ, across)
        inverse = 1.0 / jnp.max(early_all[t], axis=0)
        for k in range(PEERS):
            if k < PEERS - 1:
                early_rows(t, partner(k), inverse)
            if k:
                send_rows(t * BLOCK, BLOCK, DATA_EARLY[t], k - 1)

    arrive(HZ)
    full_all[u] = jnp.maximum(half_out[...], half_in[...])
    for k in near:
        remote(full_all.at[u], full_all.at[u], FULL, {"shard": partner(k)})

    def inverse_of(h, tile):
        tile = jnp.where(lane % 64 < GROUPS, tile, 1.0)
        tile = 1.0 / tile
        return jnp.where(h == 0, tile, pltpu.roll(tile, 64, 1))

    def tops_of(inverse, j):
        return jnp.concatenate([inverse[:, 2 * j : 2 * j + 1], inverse[:, 2 * j + 1 : 2 * j + 2]], axis=0)

    def rest_rows(d):
        inverse = inverse_of(d // 8, full_all[d % 8])
        for j in range(EARLY // 16, ROWS // 16):
            send[d, 16 * j : 16 * j + 16, :] = (xbuf[d, 16 * j : 16 * j + 16, :] * tops_of(inverse, j)).astype(
                jnp.bfloat16
            )

    arrive(FULL)
    for k in range(PEERS):
        if k < PEERS - 1:
            rest_rows(partner(k))
        if k:
            send_rows(EARLY, REST, DATA_REST, k - 1)

    arrive(LINE)
    for k in range(1, 16):
        remote(rb.at[xx, yy, cc], rb.at[xx, yy, cc], PLANE, on_plane(k))

    mine = full_all[u]
    inverse_mine = inverse_of(zh, mine)
    for j in range(ROWS // 16):
        o_ref[16 * j : 16 * j + 16, columns] = (xbuf[s, 16 * j : 16 * j + 16, :] * tops_of(inverse_mine, j)).astype(
            jnp.bfloat16
        )
    mine = jnp.where(zh == 0, mine, pltpu.roll(mine, 64, 1))
    sub = lax.broadcasted_iota(jnp.int32, (8, 128), 0)
    for b in range(pl.cdiv(ROWS, 128)):
        row = jnp.zeros((8, 128), jnp.float32)
        for g in range(16 * b, min(16 * b + 16, GROUPS)):
            here = (lane // 8 == g - 16 * b) & (sub == lane % 8)
            row = jnp.where(here, jnp.broadcast_to(mine[:, g : g + 1], (8, 128)), row)
        width = min(128, ROWS - 128 * b)
        sc_ref[:, 128 * b : 128 * b + width] = jnp.max(row, axis=0, keepdims=True)[:, :width]

    arrive(PLANE)
    remote(rb.at[:, :, cc], rb.at[:, :, cc], OTHER, {"shard": zh * 8 + yy * 2 + 1 - cc})
    arrive(OTHER)

    def router_columns(t, carry):
        h, y, c = t // 8, (t // 2) % 4, t % 2
        rows = [rb[r % 4, y, c, h * 4 + r // 4] for r in range(16)]
        rt_ref[:, pl.ds(pl.multiple_of(t * COLS, COLS), COLS)] = jnp.concatenate(rows, axis=0).astype(jnp.bfloat16)
        return carry

    lax.fori_loop(0, PEERS, router_columns, 0)

    for kind in (*DATA_EARLY, DATA_REST):
        arrive(kind)
    for kind in range(KINDS):
        leave(kind)


def finish(o_ref, sc_ref, rt_ref, out_o, out_sc, out_rt, sem):
    copies = [
        pltpu.make_async_copy(sc_ref, out_sc, sem.at[0]),
        pltpu.make_async_copy(rt_ref, out_rt, sem.at[1]),
    ]
    for k in range(CUTS):
        rows = pl.ds(k * (ROWS // CUTS), ROWS // CUTS)
        copies.append(pltpu.make_async_copy(o_ref.at[rows], out_o.at[rows], sem.at[2 + k]))
    for c in copies:
        c.start()
    for c in copies:
        c.wait()


def per_device(train_down, router_weight, router_gain):
    keep = lambda a: pltpu.with_memory_space_constraint(a, pltpu.HBM)
    x = keep(train_down.reshape(PEERS, ROWS, COLS))
    w = keep(router_weight.reshape(1, COLS))
    g = keep(router_gain.reshape(1, COLS))
    f32, bf16 = jnp.float32, jnp.bfloat16
    dma = pltpu.SemaphoreType.DMA
    tile = lambda *n: pltpu.VMEM((*n, 8, 128), f32)
    hbm = pl.BlockSpec(memory_space=pltpu.HBM)
    vmem = pl.BlockSpec(memory_space=pltpu.VMEM)
    o, sc, rt = pl.pallas_call(
        kernel,
        out_shape=(
            pltpu.VMEM((ROWS, PEERS * COLS), bf16),
            pltpu.VMEM((1, ROWS), f32),
            pltpu.VMEM((PEERS, PEERS * COLS), bf16),
        ),
        in_specs=[hbm] * 3,
        out_specs=(vmem,) * 3,
        scratch_shapes=[
            pltpu.VMEM((PEERS, ROWS, COLS), f32),
            pltpu.VMEM((PEERS, ROWS, COLS), bf16),
            tile(STEPS), tile(STEPS, PEERS),
            tile(HALF), tile(HALF), tile(), tile(), tile(HALF),
            pltpu.VMEM((2, 1, COLS), f32),
            pltpu.VMEM((4, 4, 2, 8, 1, COLS), f32),
            dma((STEPS + PEERS // LOAD,)), dma, dma((KINDS,)), dma((KINDS,)),
        ],
        compiler_params=pltpu.CompilerParams(
            collective_id=0, has_side_effects=True, vmem_limit_bytes=40 * 2**20
        ),
        name="exchange",
    )(x, w, g)
    inside = lambda a: pltpu.with_memory_space_constraint(a, pltpu.VMEM)
    ready, scale, router = pl.pallas_call(
        finish,
        out_shape=(
            jax.ShapeDtypeStruct((ROWS, PEERS * COLS), bf16),
            jax.ShapeDtypeStruct((1, ROWS), f32),
            jax.ShapeDtypeStruct((PEERS, PEERS * COLS), bf16),
        ),
        in_specs=[vmem] * 3,
        out_specs=(hbm,) * 3,
        scratch_shapes=[dma((2 + CUTS,))],
        name="finish",
    )(inside(o), inside(sc), inside(rt))
    return ready[None], scale, router.T


def solution(mesh):
    in_specs = (P("expert", None, "shard"), P("shard", "expert"), P("shard"))
    out_specs = (P("expert", "shard", None), P("expert", "shard"), P())
    return jax.shard_map(per_device, mesh=mesh, in_specs=in_specs, out_specs=out_specs, check_vma=False)
```

time: 95.1 us -> 93 us (0.978)
  Pallas kernels: 93.5 us -> 91.4 us
    pallas_call x1, Pallas kernels: 91.7 us -> 89.6 us  [per_device(): pl.pallas_call(kernel, out_shape=(pltpu.VMEM((ROWS, PEERS * COLS), bf16),...]
where the time goes in v3:
time: 93 us; the launch traced here: 92 us
  Pallas kernels  91.4 us (98%)
    pallas_call x1, Pallas kernels, per_device(): pl.pallas_call(kernel, out_shape=(pltpu.VMEM((ROWS, PEERS * COLS), bf16),...  89.6 us

profile of v3, /device:TPU:35, one launch (start us, length us, event | category | flops | bytes accessed | tf_op | source)
XLA Modules:
  0.0 92.0 jit_solution(15647910797354740301)
XLA Ops:
  0.6 89.6 %exchange.1 = (bf16[400,4096]{1,0:T(8,128)(2,1)S(1)}, f32[1,400]{1,0:T(1,128)S(1)}, bf16[16,4096]{1,0:T(8,128)(2,1)S(1)}) custom-call(f32[16,400,256]{2,1,0:T(8,128)} %bitcast.5, f32[1,256]{1,0:T(1,128)} %bitcast.6, f32[1,256]{1,0:T(1,128)} %bitcast.7), custom_call_target="tpu_custom_call" | custom-call | tf_op jit(solution)/shard_map/exchange/pallas_call | solution.py:269
  90.2 1.8 %finish.1 = (bf16[400,4096]{1,0:T(8,128)(2,1)}, f32[1,400]{1,0:T(1,128)}, bf16[16,4096]{1,0:T(8,128)(2,1)}) custom-call(bf16[400,4096]{1,0:T(8,128)(2,1)S(1)} %get-tuple-element.9.o_ref, f32[1,400]{1,0:T(1,128)S(1)} %get-tuple-element.10.sc_ref, bf16[16,4096]{1,0:T(8,128)(2,1)S(1)} %get-tuple-element.11.rt_ref), custom_call_target="tpu_custom_call" | custom-call | tf_op jit(solution)/shard_map/finish/pallas_call | solution.py:293

commit v4 on v3

--- a/solution.py
+++ b/solution.py
@@ -11,15 +11,15 @@
 ROWS, COLS = 400, 256
 GROUPS = ROWS // 8
 BLOCK = 64
-STEPS = 2
+STEPS = 1
 EARLY = BLOCK * STEPS
 REST = ROWS - EARLY
 CUTS = 5
 LOAD = 4
-PART, HZ, FULL, DATA_REST, LINE, PLANE, OTHER = range(7)
-EARLIES = range(7, 7 + STEPS)
-DATA_EARLY = range(7 + STEPS, 7 + 2 * STEPS)
-KINDS = 7 + 2 * STEPS
+PART, HZ, FULL, DATA_REST, OVER_ZH, OVER_ZL, OVER_X, OVER_Y, OVER_CORE = range(9)
+EARLIES = range(9, 9 + STEPS)
+DATA_EARLY = range(9 + STEPS, 9 + 2 * STEPS)
+KINDS = 9 + 2 * STEPS
 FAR = [(1, dy, dc) for dy in (2, 1, 3, 0) for dc in (0, 1)]
 NEAR = [(0, dy, dc) for dy in (2, 1, 3, 0) for dc in (0, 1) if (dy, dc) != (0, 0)]
 OFFSETS = FAR + NEAR
@@ -34,30 +34,18 @@
     e, s = lax.axis_index("expert"), lax.axis_index("shard")
     zl, xx = e // 4, e % 4
     zh, yy, cc = s // 8, (s // 2) % 4, s % 2
-    zz = zh * 4 + zl
     u = s % 8
 
     def partner(k):
         dz, dy, dc = OFFSETS[k]
         return ((zh + dz) % 2) * 8 + ((yy + dy) % 4) * 2 + (cc + dc) % 2
 
-    def on_line(k):
-        z = (zz + k) % 8
-        return {"expert": (z % 4) * 4 + xx, "shard": (z // 4) * 8 + yy * 2 + cc}
-
-    def on_plane(k):
-        x, y = (xx + k // 4) % 4, (yy + k % 4) % 4
-        return {"expert": zl * 4 + x, "shard": zh * 8 + y * 2 + cc}
+    along_zl = [{"expert": (zl + k) % 4 * 4 + xx, "shard": s} for k in (2, 1, 3)]
+    along_x = [{"expert": zl * 4 + (xx + k) % 4, "shard": s} for k in (2, 1, 3)]
+    along_y = [{"shard": zh * 8 + (yy + k) % 4 * 2 + cc} for k in (2, 1, 3)]
 
     near = range(len(FAR), PEERS - 1)
     across = {"shard": (s + 8) % 16}
-
-    barrier = pltpu.get_barrier_semaphore()
-    greeted = [{"shard": partner(k)} for k in range(PEERS - 1)]
-    greeted += [on_line(k) for k in (3, 5, 2, 6, 1, 7)]
-    greeted += [on_plane(k) for k in range(4, 16)]
-    for device in greeted:
-        pl.semaphore_signal(barrier, inc=1, device_id=device, device_id_type=MESH)
 
     def load(q):
         if q < STEPS:
@@ -67,7 +55,14 @@
         return pltpu.make_async_copy(x_ref.at[here], xbuf.at[here], load_sem.at[q])
 
     loads = [load(q) for q in range(STEPS + PEERS // LOAD)]
-    for c in loads:
+    loads[0].start()
+
+    barrier = pltpu.get_barrier_semaphore()
+    greeted = [{"shard": partner(k)} for k in range(PEERS - 1)] + along_zl + along_x
+    for device in greeted:
+        pl.semaphore_signal(barrier, inc=1, device_id=device, device_id_type=MESH)
+
+    for c in loads[1:]:
         c.start()
     pltpu.make_async_copy(w_ref, wbuf.at[0], in_sem).start()
     pltpu.make_async_copy(g_ref, wbuf.at[1], in_sem).start()
@@ -102,7 +97,14 @@
         return carry
 
     part_mine[...] = jnp.zeros((HALF, 8, 128), jnp.float32)
-    early_maxima(0)
+    for t in range(STEPS):
+        early_maxima(t)
+    for q in range(PEERS // LOAD):
+        loads[STEPS + q].wait()
+        lax.fori_loop(q * LOAD, q * LOAD + LOAD, rest_maxima, 0)
+    part_all[u] = part_mine[u]
+    pltpu.make_async_copy(wbuf, wbuf, in_sem).wait()
+    rb[xx, yy, cc, zl, zh] = (wbuf[0] * wbuf[1]).astype(jnp.bfloat16).astype(jnp.float32)
 
     pl.semaphore_wait(barrier, len(greeted))
 
@@ -117,9 +119,11 @@
         HZ: half_in,
         FULL: full_all.at[pl.ds(0, HALF - 1)],
         DATA_REST: send.at[pl.ds(0, PEERS - 1), pl.ds(0, REST)],
-        LINE: rb.at[0, 0, 0, pl.ds(0, 7)],
-        PLANE: xbuf.at[0, pl.ds(0, 15 * 8)],
-        OTHER: xbuf.at[0, pl.ds(0, 16 * 8)],
+        OVER_ZH: rb.at[0, 0, 0, 0, 0],
+        OVER_ZL: rb.at[0, 0, 0, pl.ds(0, 3)],
+        OVER_X: xbuf.at[0, pl.ds(0, 3 * 8)],
+        OVER_Y: xbuf.at[0, pl.ds(0, 3 * 32)],
+        OVER_CORE: xbuf.at[0, pl.ds(0, 128)],
     }
 
     for t in range(STEPS):
@@ -132,22 +136,20 @@
     def leave(kind):
         pltpu.make_async_copy(amount[kind], amount[kind], sent.at[kind]).wait()
 
-    for t in range(STEPS):
-        if t:
-            early_maxima(t)
-        for k in range(PEERS - 1):
-            remote(early_mine.at[t], early_all.at[t, s], EARLIES[t], {"shard": partner(k)})
-
-    for q in range(PEERS // LOAD):
-        loads[STEPS + q].wait()
-        lax.fori_loop(q * LOAD, q * LOAD + LOAD, rest_maxima, 0)
-    part_all[u] = part_mine[u]
+    def send_tile(t, k):
+        remote(early_mine.at[t], early_all.at[t, s], EARLIES[t], {"shard": partner(k)})
+
+    for k in range(len(FAR)):
+        send_tile(0, k)
     for k in near:
         remote(part_mine.at[partner(k) % 8], part_all.at[u], PART, {"shard": partner(k)})
-    pltpu.make_async_copy(wbuf, wbuf, in_sem).wait()
-    rb[xx, yy, cc, zz] = (wbuf[0] * wbuf[1]).astype(jnp.bfloat16).astype(jnp.float32)
-    for k in range(1, 8):
-        remote(rb.at[xx, yy, cc, zz], rb.at[xx, yy, cc, zz], LINE, on_line(k))
+    for k in near:
+        send_tile(0, k)
+    for t in range(1, STEPS):
+        for k in range(PEERS - 1):
+            send_tile(t, k)
+    own = rb.at[xx, yy, cc, zl, zh]
+    remote(own, own, OVER_ZH, across)
 
     def early_rows(t, d, inverse):
         for j in range(BLOCK // 16):
@@ -164,12 +166,12 @@
         d = partner(k)
         remote(send.at[d, pl.ds(lo, count)], o_ref.at[pl.ds(lo, count), columns], kind, {"shard": d})
 
+    arrive(PART)
+    half_out[...] = jnp.max(part_all[...], axis=0)
+    remote(half_out, half_in, HZ, across)
+
     for t in range(STEPS):
         arrive(EARLIES[t])
-        if t == 0:
-            arrive(PART)
-            half_out[...] = jnp.max(part_all[...], axis=0)
-            remote(half_out, half_in, HZ, across)
         inverse = 1.0 / jnp.max(early_all[t], axis=0)
         for k in range(PEERS):
             if k < PEERS - 1:
@@ -177,6 +179,13 @@
             if k:
                 send_rows(t * BLOCK, BLOCK, DATA_EARLY[t], k - 1)
 
+    def pass_on(kind, part, devices):
+        for device in devices:
+            remote(part, part, kind, device)
+
+    arrive(OVER_ZH)
+    pass_on(OVER_ZL, rb.at[xx, yy, cc, zl], along_zl)
+
     arrive(HZ)
     full_all[u] = jnp.maximum(half_out[...], half_in[...])
     for k in near:
@@ -204,9 +213,8 @@
         if k:
             send_rows(EARLY, REST, DATA_REST, k - 1)
 
-    arrive(LINE)
-    for k in range(1, 16):
-        remote(rb.at[xx, yy, cc], rb.at[xx, yy, cc], PLANE, on_plane(k))
+    arrive(OVER_ZL)
+    pass_on(OVER_X, rb.at[xx, yy, cc], along_x)
 
     mine = full_all[u]
     inverse_mine = inverse_of(zh, mine)
@@ -214,6 +222,9 @@
         o_ref[16 * j : 16 * j + 16, columns] = (xbuf[s, 16 * j : 16 * j + 16, :] * tops_of(inverse_mine, j)).astype(
             jnp.bfloat16
         )
+    arrive(OVER_X)
+    pass_on(OVER_Y, rb.at[:, yy, cc], along_y)
+
     mine = jnp.where(zh == 0, mine, pltpu.roll(mine, 64, 1))
     sub = lax.broadcasted_iota(jnp.int32, (8, 128), 0)
     for b in range(pl.cdiv(ROWS, 128)):
@@ -224,13 +235,13 @@
         width = min(128, ROWS - 128 * b)
         sc_ref[:, 128 * b : 128 * b + width] = jnp.max(row, axis=0, keepdims=True)[:, :width]
 
-    arrive(PLANE)
-    remote(rb.at[:, :, cc], rb.at[:, :, cc], OTHER, {"shard": zh * 8 + yy * 2 + 1 - cc})
-    arrive(OTHER)
+    arrive(OVER_Y)
+    pass_on(OVER_CORE, rb.at[:, :, cc], [{"shard": zh * 8 + yy * 2 + 1 - cc}])
+    arrive(OVER_CORE)
 
     def router_columns(t, carry):
         h, y, c = t // 8, (t // 2) % 4, t % 2
-        rows = [rb[r % 4, y, c, h * 4 + r // 4] for r in range(16)]
+        rows = [rb[r % 4, y, c, r // 4, h] for r in range(16)]
         rt_ref[:, pl.ds(pl.multiple_of(t * COLS, COLS), COLS)] = jnp.concatenate(rows, axis=0).astype(jnp.bfloat16)
         return carry
 
@@ -281,7 +292,7 @@
             tile(STEPS), tile(STEPS, PEERS),
             tile(HALF), tile(HALF), tile(), tile(), tile(HALF),
             pltpu.VMEM((2, 1, COLS), f32),
-            pltpu.VMEM((4, 4, 2, 8, 1, COLS), f32),
+            pltpu.VMEM((4, 4, 2, 4, 2, 1, COLS), f32),
             dma((STEPS + PEERS // LOAD,)), dma, dma((KINDS,)), dma((KINDS,)),
         ],
         compiler_params=pltpu.CompilerParams(

time: 93 us -> 91.8 us (0.987)
  no operation moved by 1% of the time
where the time goes in v4:
time: 91.8 us; the launch traced here: 91.7 us
  Pallas kernels  91 us (99%)
    pallas_call x1, Pallas kernels, per_device(): pl.pallas_call(kernel, out_shape=(pltpu.VMEM((ROWS, PEERS * COLS), bf16),...  89.2 us

profile of v4, /device:TPU:35, one launch (start us, length us, event | category | flops | bytes accessed | tf_op | source)
XLA Modules:
  0.0 91.7 jit_solution(5323929209241823924)
XLA Ops:
  0.6 89.2 %exchange.1 = (bf16[400,4096]{1,0:T(8,128)(2,1)S(1)}, f32[1,400]{1,0:T(1,128)S(1)}, bf16[16,4096]{1,0:T(8,128)(2,1)S(1)}) custom-call(f32[16,400,256]{2,1,0:T(8,128)} %bitcast.5, f32[1,256]{1,0:T(1,128)} %bitcast.6, f32[1,256]{1,0:T(1,128)} %bitcast.7), custom_call_target="tpu_custom_call" | custom-call | tf_op jit(solution)/shard_map/exchange/pallas_call | solution.py:280
  89.9 1.8 %finish.1 = (bf16[400,4096]{1,0:T(8,128)(2,1)}, f32[1,400]{1,0:T(1,128)}, bf16[16,4096]{1,0:T(8,128)(2,1)}) custom-call(bf16[400,4096]{1,0:T(8,128)(2,1)S(1)} %get-tuple-element.9.o_ref, f32[1,400]{1,0:T(1,128)S(1)} %get-tuple-element.10.sc_ref, bf16[16,4096]{1,0:T(8,128)(2,1)S(1)} %get-tuple-element.11.rt_ref), custom_call_target="tpu_custom_call" | custom-call | tf_op jit(solution)/shard_map/finish/pallas_call | solution.py:304

commit v5 on v4

--- a/solution.py
+++ b/solution.py
@@ -14,7 +14,7 @@
 STEPS = 1
 EARLY = BLOCK * STEPS
 REST = ROWS - EARLY
-CUTS = 5
+CUTS = 2
 LOAD = 4
 PART, HZ, FULL, DATA_REST, OVER_ZH, OVER_ZL, OVER_X, OVER_Y, OVER_CORE = range(9)
 EARLIES = range(9, 9 + STEPS)
@@ -38,7 +38,7 @@
 
     def partner(k):
         dz, dy, dc = OFFSETS[k]
-        return ((zh + dz) % 2) * 8 + ((yy + dy) % 4) * 2 + (cc + dc) % 2
+        return ((zh + dz) % 2) * 8 + ((yy + dy * (1 + 2 * cc)) % 4) * 2 + (cc + dc) % 2
 
     along_zl = [{"expert": (zl + k) % 4 * 4 + xx, "shard": s} for k in (2, 1, 3)]
     along_x = [{"expert": zl * 4 + (xx + k) % 4, "shard": s} for k in (2, 1, 3)]
@@ -59,11 +59,11 @@
 
     barrier = pltpu.get_barrier_semaphore()
     greeted = [{"shard": partner(k)} for k in range(PEERS - 1)] + along_zl + along_x
-    for device in greeted:
+    for i, device in enumerate(greeted):
         pl.semaphore_signal(barrier, inc=1, device_id=device, device_id_type=MESH)
-
-    for c in loads[1:]:
-        c.start()
+        if i == len(FAR) - 1:
+            for c in loads[1:]:
+                c.start()
     pltpu.make_async_copy(w_ref, wbuf.at[0], in_sem).start()
     pltpu.make_async_copy(g_ref, wbuf.at[1], in_sem).start()
 
@@ -142,9 +142,9 @@
     for k in range(len(FAR)):
         send_tile(0, k)
     for k in near:
+        send_tile(0, k)
+    for k in near:
         remote(part_mine.at[partner(k) % 8], part_all.at[u], PART, {"shard": partner(k)})
-    for k in near:
-        send_tile(0, k)
     for t in range(1, STEPS):
         for k in range(PEERS - 1):
             send_tile(t, k)

time: 91.8 us -> 92.4 us (level)
  no operation moved by 1% of the time
where the time goes in v5:
time: 92.4 us; the launch traced here: 91.7 us
  Pallas kernels  91 us (98%)
    pallas_call x1, Pallas kernels, per_device(): pl.pallas_call(kernel, out_shape=(pltpu.VMEM((ROWS, PEERS * COLS), bf16),...  89.2 us

profile of v5, /device:TPU:35, one launch (start us, length us, event | category | flops | bytes accessed | tf_op | source)
XLA Modules:
  0.0 91.7 jit_solution(5314222321006456022)
XLA Ops:
  0.6 89.2 %exchange.1 = (bf16[400,4096]{1,0:T(8,128)(2,1)S(1)}, f32[1,400]{1,0:T(1,128)S(1)}, bf16[16,4096]{1,0:T(8,128)(2,1)S(1)}) custom-call(f32[16,400,256]{2,1,0:T(8,128)} %bitcast.5, f32[1,256]{1,0:T(1,128)} %bitcast.6, f32[1,256]{1,0:T(1,128)} %bitcast.7), custom_call_target="tpu_custom_call" | custom-call | tf_op jit(solution)/shard_map/exchange/pallas_call | solution.py:280
  89.9 1.8 %finish.1 = (bf16[400,4096]{1,0:T(8,128)(2,1)}, f32[1,400]{1,0:T(1,128)}, bf16[16,4096]{1,0:T(8,128)(2,1)}) custom-call(bf16[400,4096]{1,0:T(8,128)(2,1)S(1)} %get-tuple-element.9.o_ref, f32[1,400]{1,0:T(1,128)S(1)} %get-tuple-element.10.sc_ref, bf16[16,4096]{1,0:T(8,128)(2,1)S(1)} %get-tuple-element.11.rt_ref), custom_call_target="tpu_custom_call" | custom-call | tf_op jit(solution)/shard_map/finish/pallas_call | solution.py:304
